TPU v7x, 32 devices: a whole 2x2x4 slice. The times are simulated.
32 devices in a mesh: tp: 4 (over z), dp: 8 (over y, x, core).
Axes of the slice: x: 2, y: 2, z: 4, core: 2. Of those that a mesh axis runs over, the one named last changes fastest.
Arguments:
- w_in: float32 [1, 1408, 10368], P(None, None, 'tp')
- w_out: float32 [1, 7552, 1408], P(None, 'tp')
- g_in: float32 [8, 1, 1408, 10368], P('dp', None, None, 'tp')
- g_out: float32 [8, 1, 7552, 1408], P('dp', None, 'tp')
- m_in: bfloat16 [1, 1408, 10368], P(None, 'dp', 'tp')
- m_out: bfloat16 [1, 7552, 1408], P(None, 'tp', 'dp')
- r_in: float32 [1, 1408], P(None, 'dp')
- c_in: float32 [1, 10368], P(None, 'tp')
- r_out: float32 [1, 7552], P(None, 'tp')
- c_out: float32 [1, 1408], P(None, 'dp')
- learn_rate: float32 [], replicated
- weight_decay: float32 [], replicated
- beta_two: float32 [], replicated
Outputs:
- output 1: float32 [1, 1408, 10368], P(None, None, 'tp')
- output 2: float32 [1, 7552, 1408], P(None, 'tp')
- output 3: bfloat16 [1, 1408, 10368], P(None, 'dp', 'tp')
- output 4: bfloat16 [1, 7552, 1408], P(None, 'tp', 'dp')
- output 5: float32 [1, 1408], P(None, 'dp')
- output 6: float32 [1, 10368], P(None, 'tp')
- output 7: float32 [1, 7552], P(None, 'tp')
- output 8: float32 [1, 1408], P(None, 'dp')
All inputs are finite; a program needn't handle non-finite values.
Results may differ from a plain program's by a relative error of at most 0.00125668.
Values sent between devices are 32-bit elements.
A program may use at most 1 GiB of HBM per device.

v0:
```python
import jax
import jax.numpy as jnp
from jax import lax
from jax.sharding import PartitionSpec as P


def local_update(weight, grad_rep, moment, row_old, col_old, learn_rate, weight_decay, beta_two, row_axis, col_axis, row_devs, col_devs):
    dp_dim = 1 if row_axis == 'dp' else 2
    grad_part = lax.psum_scatter(grad_rep[0], 'dp', scatter_dimension=dp_dim, tiled=True)
    n_rows = grad_part.shape[1] * row_devs
    n_cols = grad_part.shape[2] * col_devs
    grad_sq = grad_part * grad_part + 1e-30
    row_mean = lax.psum(jnp.sum(grad_sq, axis=2), col_axis) / n_cols
    col_mean = lax.psum(jnp.sum(grad_sq, axis=1), row_axis) / n_rows
    row_new = beta_two * row_old + (1.0 - beta_two) * row_mean
    col_new = beta_two * col_old + (1.0 - beta_two) * col_mean
    row_avg = lax.psum(jnp.sum(row_new, axis=1), row_axis) / n_rows
    second = row_new[:, :, None] * col_new[:, None, :] / row_avg[:, None, None]
    update = grad_part / jnp.sqrt(second)
    total_sq = lax.psum(jnp.sum(update * update, axis=(1, 2)), ('tp', 'dp'))
    rms_val = jnp.sqrt(total_sq / (n_rows * n_cols))
    update = update / jnp.maximum(1.0, rms_val)[:, None, None]
    mom_new = (0.9 * moment.astype(jnp.float32) + 0.1 * update).astype(jnp.bfloat16)
    width = grad_part.shape[dp_dim]
    w_block = lax.dynamic_slice_in_dim(weight, lax.axis_index('dp') * width, width, axis=dp_dim)
    w_block = w_block - learn_rate * mom_new.astype(jnp.float32) - learn_rate * weight_decay * w_block
    w_new = lax.all_gather(w_block, 'dp', axis=dp_dim, tiled=True)
    return w_new, mom_new, row_new, col_new


def solution(mesh):
    tp_devs = mesh.shape['tp']
    dp_devs = mesh.shape['dp']

    def body(w_in, w_out, g_in, g_out, m_in, m_out, r_in, c_in, r_out, c_out, learn_rate, weight_decay, beta_two):
        in_result = local_update(w_in, g_in, m_in, r_in, c_in, learn_rate, weight_decay, beta_two, 'dp', 'tp', dp_devs, tp_devs)
        out_result = local_update(w_out, g_out, m_out, r_out, c_out, learn_rate, weight_decay, beta_two, 'tp', 'dp', tp_devs, dp_devs)
        return (in_result[0], out_result[0], in_result[1], out_result[1], in_result[2], in_result[3], out_result[2], out_result[3])

    in_specs = (P(None, None, 'tp'), P(None, 'tp', None), P('dp', None, None, 'tp'), P('dp', None, 'tp', None), P(None, 'dp', 'tp'), P(None, 'tp', 'dp'), P(None, 'dp'), P(None, 'tp'), P(None, 'tp'), P(None, 'dp'), P(), P(), P())
    out_specs = (P(None, None, 'tp'), P(None, 'tp', None), P(None, 'dp', 'tp'), P(None, 'tp', 'dp'), P(None, 'dp'), P(None, 'tp'), P(None, 'tp'), P(None, 'dp'))
    return jax.shard_map(body, mesh=mesh, in_specs=in_specs, out_specs=out_specs, check_vma=False)
```

profile of v0, /device:TPU:0, one launch (start us, length us, event | category | flops | bytes accessed | tf_op | source)
XLA Modules:
  0.0 478.8 jit_solution(14360609612821682538)
XLA Ops:
  7.2 11.7 %copy.24 = f32[1,1,1888,1408]{2,3,1,0:T(8,128)} copy(f32[1,1,1888,1408]{3,2,1,0:T(8,128)} %param.16) | data formatting | bytes 21266432 | tf_op args[3]
  19.0 16.6 %copy.22 = f32[1,1,1408,2592]{3,2,1,0:T(8,128)} copy(f32[1,1,1408,2592]{2,3,1,0:T(8,128)} %param.15) | data formatting | bytes 29196288 | tf_op args[2]
  37.6 2.4 constant_dynamic-slice_fusion
  40.0 1.7 copy.28
  41.7 62.4 %reduce-scatter.5.cloned.1.call-done = f32[1,1888,176]{1,2,0:T(8,128)} async-done(((f32[1,1888,1408]{1,2,0:T(8,128)}), f32[1,1888,176]{1,2,0:T(8,128)}) %reduce-scatter.5.cloned.1.call-update) | async-done | bytes 1329168 | tf_op jit(solution)/shard_map/reduce_scatter | solution.py:9
  104.1 1.6 fusion.2
  105.8 104.9 %reduce-scatter.3.cloned.1.call-done = f32[1,176,2592]{2,1,0:T(8,128)} async-done(((f32[1,1408,2592]{2,1,0:T(8,128)}), f32[1,176,2592]{2,1,0:T(8,128)}) %reduce-scatter.3.cloned.1.call-update) | async-done | bytes 1824784 | tf_op jit(solution)/shard_map/reduce_scatter | solution.py:9
  210.8 2.1 fusion
  212.9 11.7 %psum.56 = f32[1,176]{1,0:T(1,128)S(1)} all-reduce(f32[1,176]{1,0:T(1,128)S(1)} %bitcast.20), channel_id=1, replica_groups=mesh['tp'=4,'dp'=8] {'tp'}, use_global_device_ids=true, to_apply=%region_2.0 | all-reduce | flops 176 | bytes 1408 | tf_op jit(solution)/shard_map/psum | solution.py:13
  225.2 23.4 %all-reduce.1 = (f32[1]{0:T(128)}, f32[1,2592]{1,0:T(1,128)S(1)}, f32[1,1888]{1,0:T(1,128)S(1)}) all-reduce(f32[1]{0:T(128)} %bitcast.3, f32[1,2592]{1,0:T(1,128)S(1)} %reduce_sum.91, f32[1,1888]{1,0:T(1,128)S(1)} %reduce_sum.97), channel_id=1, replica_groups=mesh['tp'=4,'dp'=8] {'dp'}, use_global_device_ids=true, to_apply=%region_6.0 | all-reduce | flops 4481 | bytes 35848 | tf_op jit(solution)/shard_map/psum | solution.py:17
  249.2 0.6 fusion.5
  249.8 1.2 fusion.4
  251.0 9.0 %all-reduce.2 = (f32[1]{0:T(128)}, f32[1,176]{1,0:T(1,128)S(1)}) all-reduce(f32[1]{0:T(128)} %bitcast.10, f32[1,176]{1,0:T(1,128)S(1)} %bitcast.21), channel_id=1, replica_groups=mesh['tp'=4,'dp'=8] {'tp'}, use_global_device_ids=true, to_apply=%region_15.0 | all-reduce | flops 177 | bytes 1416 | tf_op jit(solution)/shard_map/psum | solution.py:17
  260.7 1.2 multiply_reduce_fusion
  261.9 1.2 multiply_reduce_fusion.1
  263.1 39.9 %all-reduce = (f32[1]{0:T(128)}, f32[1]{0:T(128)}) all-reduce(f32[1]{0:T(128)} %bitcast.5, f32[1]{0:T(128)} %bitcast.12), channel_id=1, replica_groups=mesh['tp'=4,'dp'=8] {'tp','dp'}, use_global_device_ids=true, to_apply=%region_8.0 | all-reduce | flops 2 | bytes 16 | tf_op jit(solution)/shard_map/psum | solution.py:20
  303.7 3.5 multiply_subtract_fusion.1
  307.2 4.4 constant_dynamic-slice_fusion.1
  311.6 3.2 copy.27
  315.4 4.0 multiply_subtract_fusion
  319.4 51.4 %all-gather.5.cloned.1.call-done = f32[1,1888,1408]{1,2,0:T(8,128)} async-done(((f32[1,1888,176]{1,2,0:T(8,128)}), f32[1,1888,1408]{1,2,0:T(8,128)}) %all-gather.5.cloned.1.call-update) | async-done | bytes 10633232 | tf_op jit(solution)/shard_map/all_gather | solution.py:27
  370.9 11.6 %copy.26 = f32[1,1888,1408]{2,1,0:T(8,128)} copy(f32[1,1888,1408]{1,2,0:T(8,128)} %all-gather.5.cloned.1.call-done) | data formatting | bytes 21266432
  382.5 73.4 %all-gather.3.cloned.1.call-done = f32[1,1408,2592]{2,1,0:T(8,128)} async-done(((f32[1,176,2592]{2,1,0:T(8,128)}), f32[1,1408,2592]{2,1,0:T(8,128)}) %all-gather.3.cloned.1.call-update) | async-done | bytes 14598160 | tf_op jit(solution)/shard_map/all_gather | solution.py:27
  455.9 16.4 %copy.25 = f32[1,1408,2592]{1,2,0:T(8,128)} copy(f32[1,1408,2592]{2,1,0:T(8,128)} %all-gather.3.cloned.1.call-done) | data formatting | bytes 29196288
  (30 shorter events, 0.9 us)
Async XLA Ops:
  7.2 97.0 %reduce-scatter.5.cloned.1.call-start = ((), (), s32[]{:S(2)}) async-start(), calls=%async_computation.4 | async-start | bytes 12165120 | tf_op jit(solution)/shard_map/reduce_scatter | solution.py:9
  18.9 191.8 %reduce-scatter.3.cloned.1.call-start = ((), (), s32[]{:S(2)}) async-start(), calls=%async_computation.2 | async-start | bytes 17031168 | tf_op jit(solution)/shard_map/reduce_scatter | solution.py:9
  35.6 335.2 %all-gather.5.cloned.1.call-start = ((), (), s32[]{:S(2)}) async-start(), calls=%async_computation.5 | async-start | bytes 12165120 | tf_op jit(solution)/shard_map/all_gather | solution.py:27
  41.7 182.8 %copy-start.7 = (f32[1,176]{1,0:T(1,128)S(1)}, f32[1,176]{1,0:T(1,128)}, u32[]{:S(2)}) copy-start(f32[1,176]{1,0:T(1,128)} %param.19) | copy-start | bytes 2116
  41.7 207.5 %copy-start.3 = (f32[1,2592]{1,0:T(1,128)S(1)}, f32[1,2592]{1,0:T(1,128)}, u32[]{:S(2)}) copy-start(f32[1,2592]{1,0:T(1,128)} %param.20) | copy-start | bytes 31108
  41.7 208.1 %copy-start.6 = (f32[1,1888]{1,0:T(1,128)S(1)}, f32[1,1888]{1,0:T(1,128)}, u32[]{:S(2)}) copy-start(f32[1,1888]{1,0:T(1,128)} %param.21) | copy-start | bytes 22660
  41.7 218.9 %copy-start.8 = (f32[1,176]{1,0:T(1,128)S(1)}, f32[1,176]{1,0:T(1,128)}, u32[]{:S(2)}) copy-start(f32[1,176]{1,0:T(1,128)} %param.22) | copy-start | bytes 2116
  210.8 49.9 %copy-start = (f32[1,176,2592]{2,1,0:T(8,128)S(1)}, f32[1,176,2592]{2,1,0:T(8,128)}, u32[]{:S(2)}) copy-start(f32[1,176,2592]{2,1,0:T(8,128)} %reduce-scatter.3.cloned.1.call-done) | copy-start | bytes 5474308
  210.8 51.2 %copy-start.1 = (f32[1,1888,176]{1,2,0:T(8,128)S(1)}, f32[1,1888,176]{1,2,0:T(8,128)}, u32[]{:S(2)}) copy-start(f32[1,1888,176]{1,2,0:T(8,128)} %reduce-scatter.5.cloned.1.call-done) | copy-start | bytes 3987460
  225.2 90.3 %copy-start.4 = (f32[1,176]{1,0:T(1,128)}, f32[1,176]{1,0:T(1,128)S(1)}, u32[]{:S(2)}) copy-start(f32[1,176]{1,0:T(1,128)S(1)} %get-tuple-element.37) | copy-start | bytes 2116
  260.7 46.5 %copy-start.5 = (f32[1,176]{1,0:T(1,128)}, f32[1,176]{1,0:T(1,128)S(1)}, u32[]{:S(2)}) copy-start(f32[1,176]{1,0:T(1,128)S(1)} %multiply_add_fusion.4) | copy-start | bytes 2116
  307.2 148.7 %all-gather.3.cloned.1.call-start = ((), (), s32[]{:S(2)}) async-start(), calls=%async_computation.3 | async-start | bytes 17031168 | tf_op jit(solution)/shard_map/all_gather | solution.py:27
  311.6 3.8 copy-start.2
Sparse Core Ops, SparseCore 0:
  19.1 85.0 reduce-scatter.4
  107.7 102.9 reduce-scatter.2
  307.3 63.5 all-gather.4
  373.2 82.6 all-gather.2
where the time goes:
time: 480 us; the launch traced here: 479 us
  waiting for transfers between devices  292 us (61%)
  blocking collectives  83.9 us (17%)
  local copies, waits for them, and re-layouts  68 us (14%)
  between operations  18.4 us (4%)
  other arithmetic  16 us (3%)
    reduce_scatter x2, waiting for transfers between devices, local_update(): lax.psum_scatter(grad_rep[0], 'dp', scatter_dimension=dp_dim, tiled=True)  167 us
    all_gather x2, waiting for transfers between devices, local_update(): w_new = lax.all_gather(w_block, 'dp', axis=dp_dim, tiled=True)  125 us
    unnamed x24, local copies, waits for them, and re-layouts  61.3 us
    psum x1, blocking collectives, local_update(): total_sq = lax.psum(jnp.sum(update * update, axis=(1, 2)), ('tp', 'dp'))  39.9 us
    psum x2, blocking collectives, local_update(): row_avg = lax.psum(jnp.sum(row_new, axis=1), row_axis) / n_rows  32.3 us
    psum x1, blocking collectives, local_update(): row_mean = lax.psum(jnp.sum(grad_sq, axis=2), col_axis) / n_cols  11.7 us
  transfers between devices with their start and end apart: 4, of which 4 were waited for; matrix products, arithmetic and copies ran while one was open for 10% of the time, Pallas kernels for 0%

commit v1 on v0

v1 whole, which is shorter than its diff:
```python
import functools
import jax
import jax.numpy as jnp
from jax import lax
from jax.experimental import pallas as pl
from jax.experimental.pallas import tpu as pltpu
from jax.sharding import PartitionSpec as P

F32 = jnp.float32
MESH = pl.DeviceIdType.MESH


def row_cuts(half):
    cuts, at = [], 0
    step = max(8, (half // 3 + 7) // 8 * 8)
    while at < half:
        cuts.append((at, min(step, half - at)))
        at += step
    return cuts


def lane_cuts(lanes, tiles):
    return [(at, min(tiles * 128, lanes - at)) for at in range(0, lanes, tiles * 128)]


def kernel(dims, lr_ref, wd_ref, b2_ref, w_in, w_out, g_in, g_out, m_in, m_out, r_in, c_in, r_out, c_out,
           w_in_new, w_out_new, m_in_new, m_out_new, r_in_new, c_in_new, r_out_new, c_out_new,
           acc_a, sib_a, one_a, two_a, wown, mom_a, acc_b, sib_b, one_b, two_b, stage, mom_b, momt_b,
           col_a, col_b, av_a, av_b, bv_a, bv_b, rb_a, rb_b, sd_a, sd_b, st_a, st_b,
           s_load, s_stage, s_misc, d_send_a, d_recv_a, d_send_b, d_recv_b, i_send_a, i_recv_a, i_send_b, i_recv_b,
           x_send_a, x_recv_a, x_send_b, x_recv_b, y_send_a, y_recv_a, y_send_b, y_recv_b, o_sem, q_send, q_recv):
    depth, lanes_a, rows_b, lanes_b, n_tp = dims
    ch = depth // 8
    half = ch // 2
    tp = lax.axis_index('tp')
    dp = lax.axis_index('dp')
    core = dp % 2
    chip = dp // 2
    chip_x = chip + 1 - 2 * (chip % 2)
    chip_y = chip + 2 - 4 * (chip // 2)
    chip_d = 3 - chip
    sib = dp + 1 - 2 * core
    dev_x = 2 * chip_x + core
    dev_y = 2 * chip_y + core
    sets = ((0, chip_x, dev_x, chip_y, dev_y), (half, chip_y, dev_y, chip_x, dev_x))
    cuts = row_cuts(half)
    n_cut = len(cuts)
    order = [[chip_d, chip_x, chip_y, chip], [chip_d, chip_y, chip_x, chip]]

    def remote(src, dst, ssem, rsem, dev):
        return pltpu.make_async_remote_copy(src_ref=src, dst_ref=dst, send_sem=ssem, recv_sem=rsem,
                                            device_id={'dp': dev}, device_id_type=MESH)

    def remote_tp(src, dst, ssem, rsem, dev):
        return pltpu.make_async_remote_copy(src_ref=src, dst_ref=dst, send_sem=ssem, recv_sem=rsem,
                                            device_id={'tp': dev}, device_id_type=MESH)

    def load_a(st, u):
        h0 = sets[st][0]
        slot = order[st][u]
        return pltpu.make_async_copy(g_in.at[pl.ds((2 * slot + core) * ch + h0, half)],
                                     acc_a.at[slot, pl.ds(h0, half)], s_load.at[st * 4 + u])

    for u in range(4):
        for st in range(2):
            load_a(st, u).start()
    blocks = lane_cuts(rows_b, 1)
    n_stage = stage.shape[0]

    def load_stage(src, j):
        at, num = blocks[j]
        return pltpu.make_async_copy(src.at[pl.ds(at, num)], stage.at[j % n_stage, pl.ds(0, num)], s_stage.at[j % n_stage])

    for j in range(min(n_stage, len(blocks))):
        load_stage(g_out, j).start()
    ld_w = pltpu.make_async_copy(w_in.at[pl.ds(dp * ch, ch)], wown, s_misc.at[0])
    ld_ma = pltpu.make_async_copy(m_in, mom_a, s_misc.at[1])
    ld_mb = pltpu.make_async_copy(m_out, mom_b.at[pl.ds(0, rows_b)], s_misc.at[2])

    barrier = pltpu.get_barrier_semaphore()
    for d in range(1, 8):
        pl.semaphore_signal(barrier, inc=1, device_id={'dp': (dp + d) % 8}, device_id_type=MESH)
    for d in range(1, n_tp):
        pl.semaphore_signal(barrier, inc=1, device_id={'tp': (tp + d) % n_tp}, device_id_type=MESH)
    pl.semaphore_wait(barrier, 7 + n_tp - 1)

    def d2d_a(st, u, c, other):
        h0 = sets[st][0]
        slot = order[st][u]
        at, num = cuts[c]
        i = (st * 4 + u) * n_cut + c
        return remote(g_in.at[pl.ds((2 * slot + 1 - core) * ch + h0 + at, num)],
                      sib_a.at[slot, pl.ds(h0 + at, num)], d_send_a.at[i], d_recv_a.at[i], sib)

    def d2d_b(st, u, other):
        h0 = sets[st][0]
        slot = order[st][u]
        i = st * 4 + u
        return remote(acc_b.at[pl.ds((2 * slot + 1 - core) * ch + h0, half)],
                      sib_b.at[slot, pl.ds(h0, half)], d_send_b.at[i], d_recv_b.at[i], sib)

    for u in range(4):
        for c in range(n_cut):
            for st in range(2):
                d2d_a(st, u, c, True).start()
    ld_w.start()
    ld_ma.start()
    ld_mb.start()

    def view_a(slot, r0, num):
        return acc_a.at[slot, pl.ds(r0, num)]

    def view_b(slot, r0, num):
        return acc_b.at[pl.ds((2 * slot + core) * ch + r0, num)]

    def add(dst, src, num):
        def step(i, carry):
            r = pl.ds(pl.multiple_of(i * 8, 8), 8)
            dst[r, :] = dst[r, :] + src[r, :]
            return carry
        lax.fori_loop(0, num // 8, step, 0)

    class Mat:
        pass

    a, b = Mat(), Mat()
    a.view, a.one, a.two, a.isend, a.irecv, a.sibling = view_a, one_a, two_a, i_send_a, i_recv_a, sib_a
    b.view, b.one, b.two, b.isend, b.irecv, b.sibling = view_b, one_b, two_b, i_send_b, i_recv_b, sib_b

    def hop(m, st, u, c):
        h0, c1, dev1, c2, dev2 = sets[st]
        at, num = cuts[c]
        i = (st * 3 + u) * n_cut + c
        if u == 0:
            src, dst, dev = m.view(chip_d, h0 + at, num), m.one.at[st, 0, pl.ds(at, num)], dev1
        elif u == 1:
            src, dst, dev = m.view(c1, h0 + at, num), m.one.at[st, 1, pl.ds(at, num)], dev1
        else:
            src, dst, dev = m.view(c2, h0 + at, num), m.two.at[st, pl.ds(at, num)], dev2
        return remote(src, dst, m.isend.at[i], m.irecv.at[i], dev)

    def pair_up(m, st, u, c):
        h0 = sets[st][0]
        slot = order[st][u]
        at, num = cuts[c]
        if m is a:
            if c == 0:
                load_a(st, u).wait()
            d2d_a(st, u, c, False).wait_recv()
        elif c == 0:
            d2d_b(st, u, False).wait_recv()
        add(m.view(slot, h0 + at, num), m.sibling.at[slot, pl.ds(h0 + at, num)], num)

    def first(m, u):
        for c in range(n_cut):
            for st in range(2):
                pair_up(m, st, u, c)
            for st in range(2):
                hop(m, st, u, c).start()

    def settle(m):
        for u in (2, 3):
            for c in range(n_cut):
                for st in range(2):
                    pair_up(m, st, u, c)

    def second(m):
        for c in range(n_cut):
            at, num = cuts[c]
            for st in range(2):
                hop(m, st, 0, c).wait_recv()
                add(m.view(sets[st][3], sets[st][0] + at, num), m.one.at[st, 0, pl.ds(at, num)], num)
            for st in range(2):
                hop(m, st, 2, c).start()

    def finish(m):
        for u, buf in ((1, m.one), (2, m.two)):
            for c in range(n_cut):
                at, num = cuts[c]
                for st in range(2):
                    hop(m, st, u, c).wait_recv()
                    src = m.one.at[st, 1, pl.ds(at, num)] if u == 1 else m.two.at[st, pl.ds(at, num)]
                    add(m.view(chip, sets[st][0] + at, num), src, num)
        for u in range(3):
            for c in range(n_cut):
                for st in range(2):
                    hop(m, st, u, c).wait_send()
        for u in range(4):
            for st in range(2):
                if m is a:
                    for c in range(n_cut):
                        d2d_a(st, u, c, True).wait_send()
                else:
                    d2d_b(st, u, True).wait_send()

    def transpose_b():
        for j, (at, num) in enumerate(blocks):
            load_stage(g_out, j).wait()
            buf = stage.at[j % n_stage]
            if num < 128:
                buf[num:, :] = jnp.zeros((128 - num, depth), F32)
            acc_b[:, at:at + 128] = buf[...].T
            if j + n_stage < len(blocks):
                load_stage(g_out, j + n_stage).start()
        for u in range(4):
            for st in range(2):
                d2d_b(st, u, True).start()

    n_in, n_out = lanes_a * n_tp, rows_b * n_tp
    beta = b2_ref[0]
    a.lanes, a.valid, a.col, a.av, a.bv, a.rb, a.sd, a.st = lanes_a, lanes_a, col_a, av_a, bv_a, rb_a, sd_a, st_a
    b.lanes, b.valid, b.col, b.av, b.bv, b.rb, b.sd, b.st = lanes_b, rows_b, col_b, av_b, bv_b, rb_b, sd_b, st_b
    a.aold, a.bold, a.anew, a.bnew, a.na, a.nb, a.q = r_in, c_in, r_in_new, c_in_new, n_in, depth, 0
    b.aold, b.bold, b.anew, b.bnew, b.na, b.nb, b.q = c_out, r_out, c_out_new, r_out_new, n_out, depth, 20
    eye = lax.broadcasted_iota(jnp.int32, (ch, ch), 0) == lax.broadcasted_iota(jnp.int32, (ch, ch), 1)

    def all_dp(m, buf, base):
        return [remote(buf.at[dp], buf.at[dp], q_send.at[m.q + base + d - 1], q_recv.at[m.q + base + d - 1], (dp + d) % 8)
                for d in range(1, 8)]

    def all_tp(m, buf, base):
        return [remote_tp(buf.at[tp], buf.at[tp], q_send.at[m.q + base + d - 1], q_recv.at[m.q + base + d - 1], (tp + d) % n_tp)
                for d in range(1, n_tp)]

    def wait_dp(m, buf, base):
        for d in range(1, 8):
            src = (dp + 8 - d) % 8
            cp = remote(buf.at[src], buf.at[src], q_send.at[m.q + base + d - 1], q_recv.at[m.q + base + d - 1], src)
            cp.wait_recv()
            cp.wait_send()

    def wait_tp(m, buf, base):
        for d in range(1, n_tp):
            src = (tp + n_tp - d) % n_tp
            cp = remote_tp(buf.at[src], buf.at[src], q_send.at[m.q + base + d - 1], q_recv.at[m.q + base + d - 1], src)
            cp.wait_recv()
            cp.wait_send()

    def stat1(m):
        own = m.view(chip, 0, ch)
        eps = jnp.full((1, m.lanes), 1e-30, F32)
        if m.valid < m.lanes:
            eps = jnp.where(lax.broadcasted_iota(jnp.int32, (1, m.lanes), 1) < m.valid, eps, 0.0)

        def step(i, colsum):
            r = pl.ds(pl.multiple_of(i * 8, 8), 8)
            g = own[r, :]
            sq = g * g + eps
            m.col[r, :] = jnp.broadcast_to(jnp.sum(sq, axis=1, keepdims=True), (8, 128))
            return colsum + sq
        colsum = lax.fori_loop(0, ch // 8, step, jnp.zeros((8, m.lanes), F32))
        m.bv[dp] = jnp.sum(colsum, axis=0, keepdims=True)
        rows = jnp.broadcast_to(m.col[:, 0:1], (ch, ch))
        m.av[tp] = jnp.sum(jnp.where(eye, rows, 0.0), axis=0, keepdims=True)
        for cp in all_dp(m, m.bv, 0) + all_tp(m, m.av, 7):
            cp.start()

    def stat2(m):
        own = m.view(chip, 0, ch)
        wait_dp(m, m.bv, 0)
        wait_tp(m, m.av, 7)
        bsum = m.bv[0]
        for i in range(1, 8):
            bsum = bsum + m.bv[i]
        asum = m.av[0]
        for i in range(1, n_tp):
            asum = asum + m.av[i]
        anew = beta * m.aold[...] + (1.0 - beta) * (asum / m.na)
        bnew = beta * m.bold[...] + (1.0 - beta) * (bsum[:, :m.valid] / m.nb)
        m.anew[...] = anew
        m.bnew[...] = bnew
        if m.valid < m.lanes:
            m.rb[...] = jnp.zeros((8, m.lanes), F32)
        m.rb[:, :m.valid] = jnp.broadcast_to(1.0 / jnp.sqrt(bnew), (8, m.valid))
        ra = 1.0 / jnp.sqrt(anew)
        m.col[...] = jnp.broadcast_to(
            jnp.sum(jnp.where(eye, jnp.broadcast_to(ra, (ch, ch)), 0.0), axis=1, keepdims=True), (ch, 128))

        def step(i, total):
            r = pl.ds(pl.multiple_of(i * 8, 8), 8)
            t = own[r, :] * m.col[r, 0:1] * m.rb[...]
            own[r, :] = t
            return total + t * t
        total = lax.fori_loop(0, ch // 8, step, jnp.zeros((8, m.lanes), F32))
        total = jnp.sum(jnp.sum(total, axis=1, keepdims=True), axis=0, keepdims=True)
        rsum = jnp.sum(anew if m is a else bnew, axis=1, keepdims=True)
        lane = lax.broadcasted_iota(jnp.int32, (1, 128), 1)
        m.sd[dp] = jnp.where(lane == 0, jnp.broadcast_to(total, (1, 128)), jnp.broadcast_to(rsum, (1, 128)))
        for cp in all_dp(m, m.sd, 10):
            cp.start()

    def stat3(m):
        mine = m.sd[dp]
        wait_dp(m, m.sd, 10)
        tot = m.sd[0]
        for i in range(1, 8):
            tot = tot + m.sd[i]
        if m is b:
            lane = lax.broadcasted_iota(jnp.int32, (1, 128), 1)
            tot = jnp.where(lane == 0, tot, mine)
        m.st[tp] = tot
        for cp in all_tp(m, m.st, 17):
            cp.start()

    def factor(m):
        wait_tp(m, m.st, 17)
        mine = m.st[tp]
        tot = m.st[0]
        for i in range(1, n_tp):
            tot = tot + m.st[i]
        usum = tot[:, 0:1]
        if m is a:
            ravg = mine[:, 1:2] / depth
            count = depth * n_in
        else:
            ravg = tot[:, 1:2] / n_out
            count = depth * n_out
        rms = jnp.sqrt(ravg * usum / count)
        return jnp.sqrt(ravg) / jnp.maximum(1.0, rms)

    lr = lr_ref[0]
    decay = lr_ref[0] * wd_ref[0]

    new_a = sib_a

    def out_a(slot, r0, num, own_core):
        k = core if own_core else 1 - core
        return w_in_new.at[pl.ds((2 * slot + k) * ch + r0, num)]

    def ring(st, u, send):
        h0, c1, dev1, c2, dev2 = sets[st]
        if send:
            return (chip, dev2) if u == 0 else (chip, dev1) if u == 1 else (c2, dev1)
        return (c2, dev2) if u == 0 else (c1, dev1) if u == 1 else (chip_d, dev1)

    def x_a(st, u, c, send):
        slot, dev = ring(st, u, send)
        at, num = cuts[c]
        i = (st * 3 + u) * n_cut + c
        ref = new_a.at[slot, pl.ds(sets[st][0] + at, num)]
        return remote(ref, ref, x_send_a.at[i], x_recv_a.at[i], dev)

    def y_a(st, u, c, send):
        slot = order[st][u]
        at, num = cuts[c]
        i = (st * 4 + u) * n_cut + c
        r0 = sets[st][0] + at
        src = new_a.at[slot, pl.ds(r0, num)]
        return remote(src, out_a(slot, r0, num, send), y_send_a.at[i], y_recv_a.at[i], sib)

    def o_a(st, u, c):
        slot = order[st][u]
        at, num = cuts[c]
        i = (st * 4 + u) * n_cut + c
        r0 = sets[st][0] + at
        return pltpu.make_async_copy(new_a.at[slot, pl.ds(r0, num)], out_a(slot, r0, num, True), o_sem.at[i])

    def emit_a(st, u, c):
        y_a(st, u, c, True).start()
        o_a(st, u, c).start()

    def final_a():
        f = factor(a)
        own = view_a(chip, 0, ch)
        ld_w.wait()
        ld_ma.wait()

        def step(i, carry):
            r = pl.ds(pl.multiple_of(i * 16, 16), 16)
            u = own[r, :] * f
            mom = (0.9 * mom_a[r, :].astype(F32) + 0.1 * u).astype(jnp.bfloat16)
            mom_a[r, :] = mom
            w = wown[r, :]
            new_a[chip, r, :] = w - lr * mom.astype(F32) - decay * w
            return carry
        lax.fori_loop(0, ch // 16, step, 0)
        pltpu.make_async_copy(mom_a, m_in_new, s_misc.at[1]).start()

    def own_a(c):
        for st in range(2):
            x_a(st, 0, c, True).start()
        for st in range(2):
            x_a(st, 1, c, True).start()
        for st in range(2):
            emit_a(st, 3, c)

    def forward_a(c):
        for st in range(2):
            x_a(st, 0, c, False).wait_recv()
            x_a(st, 2, c, True).start()
            emit_a(st, 2, c)
        for st in range(2):
            x_a(st, 1, c, False).wait_recv()
            emit_a(st, 1, c)

    def last_a(c):
        for st in range(2):
            x_a(st, 2, c, False).wait_recv()
            emit_a(st, 0, c)

    def drain_a():
        for c in range(n_cut):
            for st in range(2):
                for u in range(3):
                    x_a(st, u, c, True).wait_send()
                for u in range(4):
                    y_a(st, u, c, True).wait_send()
                    y_a(st, u, c, False).wait_recv()
                    o_a(st, u, c).wait()
        pltpu.make_async_copy(mom_a, m_in_new, s_misc.at[1]).wait()

    parts = lane_cuts(lanes_b, 3)
    n_part = len(parts)

    def x_b(st, u, c, send):
        slot, dev = ring(st, u, send)
        at, num = parts[c]
        i = (st * 3 + u) * n_part + c
        ref = acc_b.at[pl.ds((2 * slot + core) * ch + sets[st][0], half), pl.ds(at, num)]
        return remote(ref, ref, x_send_b.at[i], x_recv_b.at[i], dev)

    def y_b(st, u, c, send):
        slot = order[st][u]
        at, num = parts[c]
        i = (st * 4 + u) * n_part + c
        k = core if send else 1 - core
        ref = acc_b.at[pl.ds((2 * slot + k) * ch + sets[st][0], half), pl.ds(at, num)]
        return remote(ref, ref, y_send_b.at[i], y_recv_b.at[i], sib)

    def moment_b():
        ld_mb.wait()
        if len(blocks) * 128 > rows_b:
            mom_b[rows_b:, :] = jnp.zeros((len(blocks) * 128 - rows_b, ch), jnp.bfloat16)
        for j in range(len(blocks)):
            momt_b[:, j * 128:j * 128 + 128] = mom_b[j * 128:j * 128 + 128, :].astype(F32).T

    def final_b():
        f = factor(b)
        own = view_b(chip, 0, ch)

        def step(i, carry):
            r = pl.ds(pl.multiple_of(i * 8, 8), 8)
            u = own[r, :] * f
            own[r, :] = (0.9 * momt_b[r, :] + 0.1 * u).astype(jnp.bfloat16).astype(F32)
            return carry
        lax.fori_loop(0, ch // 8, step, 0)

    def store_moment_b():
        own = view_b(chip, 0, ch)
        for j in range(len(blocks)):
            mom_b[j * 128:j * 128 + 128, :] = own[:, j * 128:j * 128 + 128].T.astype(jnp.bfloat16)
        pltpu.make_async_copy(mom_b.at[pl.ds(0, rows_b)], m_out_new, s_misc.at[2]).start()

    def own_b(c):
        for st in range(2):
            x_b(st, 0, c, True).start()
        for st in range(2):
            x_b(st, 1, c, True).start()
        for st in range(2):
            y_b(st, 3, c, True).start()

    def forward_b(c):
        for st in range(2):
            x_b(st, 0, c, False).wait_recv()
            x_b(st, 2, c, True).start()
            y_b(st, 2, c, True).start()
        for st in range(2):
            x_b(st, 1, c, False).wait_recv()
            y_b(st, 1, c, True).start()

    def last_b(c):
        for st in range(2):
            x_b(st, 2, c, False).wait_recv()
            y_b(st, 0, c, True).start()

    def put_b(j):
        at, num = blocks[j]
        return pltpu.make_async_copy(stage.at[j % n_stage, pl.ds(0, num)], w_out_new.at[pl.ds(at, num)], s_stage.at[n_stage + j % n_stage])

    def finish_b(c):
        for st in range(2):
            for u in range(4):
                y_b(st, u, c, False).wait_recv()
        at, num = parts[c]
        for j in range(at // 128, (at + num) // 128):
            load_stage(w_out, j).wait()
            buf = stage.at[j % n_stage]
            w = buf[...]
            buf[...] = w - lr * acc_b[:, j * 128:j * 128 + 128].T - decay * w
            put_b(j).start()
            nxt = j - 1 + n_stage
            if j >= 1 and nxt < len(blocks):
                put_b(j - 1).wait()
                load_stage(w_out, nxt).start()

    def drain_b():
        for c in range(n_part):
            for st in range(2):
                for u in range(3):
                    x_b(st, u, c, True).wait_send()
                for u in range(4):
                    y_b(st, u, c, True).wait_send()
        for j in range(max(0, len(blocks) - n_stage), len(blocks)):
            put_b(j).wait()
        pltpu.make_async_copy(mom_b.at[pl.ds(0, rows_b)], m_out_new, s_misc.at[2]).wait()

    first(a, 0)
    first(a, 1)
    settle(a)
    transpose_b()
    second(a)
    first(b, 0)
    moment_b()
    finish(a)
    stat1(a)
    first(b, 1)
    settle(b)
    stat2(a)
    second(b)
    stat3(a)
    final_a()
    own_a(0)
    finish(b)
    stat1(b)
    for c in range(1, n_cut):
        own_a(c)
        forward_a(c - 1)
        if c == 1:
            stat2(b)
        if c >= 2:
            last_a(c - 2)
    for j in range(min(n_stage, len(blocks))):
        load_stage(w_out, j).start()
    stat3(b)
    forward_a(n_cut - 1)
    if n_cut >= 2:
        last_a(n_cut - 2)
    final_b()
    own_b(0)
    last_a(n_cut - 1)
    store_moment_b()
    for c in range(1, n_part + 3):
        if c < n_part:
            own_b(c)
        if 0 <= c - 1 < n_part:
            forward_b(c - 1)
        if 0 <= c - 2 < n_part:
            last_b(c - 2)
        if 0 <= c - 3 < n_part:
            finish_b(c - 3)
    drain_a()
    drain_b()


def fused(dims, args):
    depth, lanes_a, rows_b, lanes_b, n_tp = dims
    ch = depth // 8
    half = ch // 2
    n_cut = len(row_cuts(half))
    n_part = len(lane_cuts(lanes_b, 3))
    n_stage = 5
    any_spec = pl.BlockSpec(memory_space=pl.ANY)
    vec = pl.BlockSpec(memory_space=pltpu.VMEM)
    smem = pl.BlockSpec(memory_space=pltpu.SMEM)
    dma = pltpu.SemaphoreType.DMA
    sh = jax.ShapeDtypeStruct
    return pl.pallas_call(
        functools.partial(kernel, dims),
        out_shape=(sh((depth, lanes_a), F32), sh((rows_b, depth), F32), sh((ch, lanes_a), jnp.bfloat16),
                   sh((rows_b, ch), jnp.bfloat16), sh((1, ch), F32), sh((1, lanes_a), F32), sh((1, rows_b), F32), sh((1, ch), F32)),
        in_specs=[smem] * 3 + [any_spec] * 6 + [vec] * 4,
        out_specs=(any_spec,) * 4 + (vec,) * 4,
        scratch_shapes=[
            pltpu.VMEM((4, ch, lanes_a), F32), pltpu.VMEM((4, ch, lanes_a), F32),
            pltpu.VMEM((2, 2, half, lanes_a), F32), pltpu.VMEM((2, half, lanes_a), F32),
            pltpu.VMEM((ch, lanes_a), F32), pltpu.VMEM((ch, lanes_a), jnp.bfloat16),
            pltpu.VMEM((depth, lanes_b), F32), pltpu.VMEM((4, ch, lanes_b), F32),
            pltpu.VMEM((2, 2, half, lanes_b), F32), pltpu.VMEM((2, half, lanes_b), F32),
            pltpu.VMEM((n_stage, 128, depth), F32), pltpu.VMEM((lanes_b, ch), jnp.bfloat16), pltpu.VMEM((ch, lanes_b), F32),
            pltpu.VMEM((ch, 128), F32), pltpu.VMEM((ch, 128), F32),
            pltpu.VMEM((n_tp + 8, 1, ch), F32), pltpu.VMEM((n_tp + 8, 1, ch), F32),
            pltpu.VMEM((9, 1, lanes_a), F32), pltpu.VMEM((9, 1, lanes_b), F32),
            pltpu.VMEM((8, lanes_a), F32), pltpu.VMEM((8, lanes_b), F32),
            pltpu.VMEM((16, 1, 128), F32), pltpu.VMEM((16, 1, 128), F32),
            pltpu.VMEM((n_tp + 8, 1, 128), F32), pltpu.VMEM((n_tp + 8, 1, 128), F32),
            dma((8,)), dma((2 * n_stage,)), dma((3,)),
            dma((8 * n_cut,)), dma((8 * n_cut,)), dma((8,)), dma((8,)),
            dma((6 * n_cut,)), dma((6 * n_cut,)), dma((6 * n_cut,)), dma((6 * n_cut,)),
            dma((6 * n_cut,)), dma((6 * n_cut,)), dma((6 * n_part,)), dma((6 * n_part,)),
            dma((8 * n_cut,)), dma((8 * n_cut,)), dma((8 * n_part,)), dma((8 * n_part,)),
            dma((8 * n_cut,)), dma((40,)), dma((40,)),
        ],
        compiler_params=pltpu.CompilerParams(collective_id=0, has_side_effects=True, vmem_limit_bytes=66 * 1000 * 1000),
    )(*args)


def solution(mesh):
    n_tp = mesh.shape['tp']

    def body(w_in, w_out, g_in, g_out, m_in, m_out, r_in, c_in, r_out, c_out, learn_rate, weight_decay, beta_two):
        depth, lanes_a = w_in.shape[1:]
        rows_b = w_out.shape[1]
        dims = (depth, lanes_a, rows_b, (rows_b + 127) // 128 * 128, n_tp)
        outs = fused(dims, (learn_rate.reshape(1), weight_decay.reshape(1), beta_two.reshape(1), w_in[0], w_out[0],
                            g_in[0, 0], g_out[0, 0], m_in[0], m_out[0], r_in, c_in, r_out, c_out))
        return tuple(o[None] for o in outs[:4]) + tuple(outs[4:])

    in_specs = (P(None, None, 'tp'), P(None, 'tp', None), P('dp', None, None, 'tp'), P('dp', None, 'tp', None), P(None, 'dp', 'tp'), P(None, 'tp', 'dp'), P(None, 'dp'), P(None, 'tp'), P(None, 'tp'), P(None, 'dp'), P(), P(), P())
    out_specs = (P(None, None, 'tp'), P(None, 'tp', None), P(None, 'dp', 'tp'), P(None, 'tp', 'dp'), P(None, 'dp'), P(None, 'tp'), P(None, 'tp'), P(None, 'dp'))
    return jax.shard_map(body, mesh=mesh, in_specs=in_specs, out_specs=out_specs, check_vma=False)
```

time: 480 us -> 298 us (0.62)
  waiting for transfers between devices: 292 us -> 0 us
  Pallas kernels: 0 us -> 229 us
  blocking collectives: 83.9 us -> 0 us
  other arithmetic: 16 us -> 0 us
  between operations: 18.4 us -> 2.62 us
    pallas_call x0 -> x1, Pallas kernels: none -> 229 us  [fused(): pl.pallas_call(functools.partial(kernel, dims), out_shape=(sh((depth, lan...]
    reduce_scatter x2 -> x0, waiting for transfers between devices: 167 us -> none  [local_update(): lax.psum_scatter(grad_rep[0], 'dp', scatter_dimension=dp_dim, tiled=True)]
    all_gather x2 -> x0, waiting for transfers between devices: 125 us -> none  [local_update(): w_new = lax.all_gather(w_block, 'dp', axis=dp_dim, tiled=True)]
    psum x4 -> x0, blocking collectives: 83.9 us -> none  [the longest x1 39.9 us: local_update(): total_sq = lax.psum(jnp.sum(update * update, axis=(1, 2)), ('tp', 'dp'))]
    sub x2 -> x0, other arithmetic: 7.44 us -> none  [local_update(): w_block - learn_rate * mom_new.astype(jnp.float32)]
    dynamic_slice x2 -> x0, local copies, waits for them, and re-layouts: 6.78 us -> none  [local_update(): lax.dynamic_slice_in_dim(weight, lax.axis_index('dp') * width, width, axi...]
    reduce_sum x5 -> x0, other arithmetic: 6.76 us -> none  [the longest x2 3.74 us: local_update(): col_mean = lax.psum(jnp.sum(grad_sq, axis=1), row_axis) / n_rows]
    unnamed x24 -> x23, local copies, waits for them, and re-layouts: 61.3 us -> 65.5 us
  transfers between devices with their start and end apart: 4 -> 0, of which waited for: 4 -> 0; matrix products, arithmetic and copies ran while one was open for 10% -> 0% of each run, Pallas kernels for 0% -> 0%
where the time goes in v1:
time: 298 us; the launch traced here: 297 us
  Pallas kernels  229 us (77%)
  local copies, waits for them, and re-layouts  65.5 us (22%)
    pallas_call x1, Pallas kernels, fused(): pl.pallas_call(functools.partial(kernel, dims), out_shape=(sh((depth, lan...  229 us
    unnamed x23, local copies, waits for them, and re-layouts  65.5 us

profile of v1, /device:TPU:0, one launch (start us, length us, event | category | flops | bytes accessed | tf_op | source)
XLA Modules:
  0.0 296.7 jit_solution(3146489620811147235)
XLA Ops:
  2.6 2.2 copy.23
  4.8 16.6 %copy.21 = f32[1,1408,2592]{2,1,0:T(8,128)} copy(f32[1,1408,2592]{1,2,0:T(8,128)} %param.13) | data formatting | bytes 29196288 | tf_op args[0]
  21.4 16.7 %copy.22 = f32[1,1,1408,2592]{3,2,1,0:T(8,128)} copy(f32[1,1,1408,2592]{2,3,1,0:T(8,128)} %param.15) | data formatting | bytes 29196288 | tf_op args[2]
  38.1 228.5 %shard_map.188 = (f32[1408,2592]{1,0:T(8,128)}, f32[1888,1408]{1,0:T(8,128)}, bf16[176,2592]{1,0:T(8,128)(2,1)}, bf16[1888,176]{1,0:T(8,128)(2,1)}, f32[1,176]{1...) custom-call(f32[1]{0:T(128)} %bitcast.13.lr_ref, f32[1]{0:T(128)} %bitcast.14.wd_ref, ...), custom_call_target="tpu_custom_call" | custom-call | tf_op jit(solution)/shard_map/pallas_call | solution.py:567
  266.6 0.0 copy-start
  266.6 16.5 %copy.24 = f32[1,1408,2592]{1,2,0:T(8,128)} copy(f32[1,1408,2592]{2,1,0:T(8,128)} %bitcast.18) | data formatting | bytes 29196288
  283.1 0.0 copy-start.1
  283.1 0.0 copy-start.5
  283.1 0.0 copy-start.2
  283.1 0.0 copy-start.3
  283.1 0.0 copy-start.4
  283.1 0.0 copy-done
  283.1 1.4 copy.25
  284.6 8.8 %copy.35 = f32[1,1888,1408]{2,1,0:T(8,128)} copy(f32[1,1888,1408]{2,1,0:T(8,128)} %bitcast.21) | data formatting | bytes 21266432
  293.4 0.0 copy-done.1
  293.4 0.9 copy.36
  294.3 0.0 copy-done.5
  294.3 0.6 copy.37
  294.9 0.0 copy-done.2
  294.9 0.6 copy.38
  295.5 0.0 copy-done.3
  295.5 0.6 copy.39
  296.1 0.0 copy-done.4
  296.1 0.6 copy.40
Async XLA Ops:
  266.6 16.5 %copy-start = (bf16[1888,176]{1,0:T(8,128)(2,1)S(1)}, bf16[1888,176]{1,0:T(8,128)(2,1)}, u32[]{:S(2)}) copy-start(bf16[1888,176]{1,0:T(8,128)(2,1)} %get-tuple-element.19) | copy-start | bytes 1993732
  283.1 10.3 %copy-start.1 = (bf16[176,2592]{1,0:T(8,128)(2,1)S(1)}, bf16[176,2592]{1,0:T(8,128)(2,1)}, u32[]{:S(2)}) copy-start(bf16[176,2592]{1,0:T(8,128)(2,1)} %get-tuple-element.18) | copy-start | bytes 2737156
  283.1 11.2 %copy-start.5 = (f32[1,176]{1,0:T(1,128)S(1)}, f32[1,176]{1,0:T(1,128)}, u32[]{:S(2)}) copy-start(f32[1,176]{1,0:T(1,128)} %get-tuple-element.44) | copy-start | bytes 2116
  283.1 11.8 %copy-start.2 = (f32[1,2592]{1,0:T(1,128)S(1)}, f32[1,2592]{1,0:T(1,128)}, u32[]{:S(2)}) copy-start(f32[1,2592]{1,0:T(1,128)} %get-tuple-element.45) | copy-start | bytes 31108
  283.1 12.4 %copy-start.3 = (f32[1,1888]{1,0:T(1,128)S(1)}, f32[1,1888]{1,0:T(1,128)}, u32[]{:S(2)}) copy-start(f32[1,1888]{1,0:T(1,128)} %get-tuple-element.46) | copy-start | bytes 22660
  283.1 13.0 %copy-start.4 = (f32[1,176]{1,0:T(1,128)S(1)}, f32[1,176]{1,0:T(1,128)}, u32[]{:S(2)}) copy-start(f32[1,176]{1,0:T(1,128)} %get-tuple-element.47) | copy-start | bytes 2116
